TPU v7x, 32 devices: a whole 2x2x4 slice. The times are simulated.
32 devices in a mesh: samp: 16 (over z, y, x), feat: 2 (over core).
Axes of the slice: x: 2, y: 2, z: 4, core: 2. Of those that a mesh axis runs over, the one named last changes fastest.
Arguments:
- design_matrix: bfloat16 [2048, 32768], P('samp', 'feat'), may hold values from -0.046875 to 0.046875
- labels: int32 [2048], P('samp'), may hold values from 0 to 1
- weights: float32 [16, 32768], P(None, ('feat', 'samp')), may hold values from -6 to 6
- lambdas: float32 [16], replicated, may hold values from 0.05 to 1
- sketch: bfloat16 [32768, 384], P(('feat', 'samp')), may hold values from -0.03125 to 0.03125
- sketch_values: float32 [384], replicated, may hold values from 0.05 to 2
Outputs:
- new_weights: float32 [16, 32768], P(None, ('feat', 'samp'))
All inputs are finite; a program needn't handle non-finite values.
Results may differ from a plain program's by a relative error of at most 0.004.
Values may be sent and summed in bfloat16 or wider, within the bound.
A program may use at most 64 MiB of HBM per device.

v0:
```python
import jax
import jax.numpy as jnp
from jax import lax
from jax.sharding import PartitionSpec as P

ITERS = 2


def shards(design_matrix, labels, weights, lambdas, sketch, sketch_values):
    sketch_full = sketch.astype(jnp.float32)
    smallest = jnp.min(sketch_values)
    ratios = (smallest + lambdas[:, None]) / (sketch_values[None, :] + lambdas[:, None]) - 1.0

    def apply_rows(vector):
        vector_half = vector.astype(jnp.bfloat16)
        partial_rows = lax.dot_general(
            lax.all_gather(vector_half, "samp", axis=1, tiled=True),
            design_matrix,
            (((1,), (1,)), ((), ())),
            preferred_element_type=jnp.float32,
        )
        return lax.psum(partial_rows, "feat")

    def apply_columns(values):
        return lax.psum_scatter(
            lax.dot_general(
                design_matrix, values, (((0,), (1,)), ((), ())), preferred_element_type=jnp.float32
            ),
            "samp",
            scatter_dimension=0,
            tiled=True,
        ).T

    def precondition(residual):
        projected = jnp.dot(residual, sketch_full, precision=lax.Precision.HIGHEST)
        projected = lax.psum(projected, ("samp", "feat"))
        correction = lax.dot_general(
            ratios * projected,
            sketch_full,
            (((1,), (1,)), ((), ())),
            precision=lax.Precision.HIGHEST,
        )
        precond_res = residual + correction
        res_dot = lax.psum(jnp.sum(residual * precond_res, axis=1), ("samp", "feat"))
        return (precond_res, res_dot)

    logits = apply_rows(weights)
    probability = jax.nn.sigmoid(logits)
    hessian_diag = probability * (1.0 - probability)
    miss_rows = (probability - labels[None, :].astype(jnp.float32)).astype(jnp.bfloat16)
    gradient = apply_columns(miss_rows) + lambdas[:, None] * weights
    residual = -gradient
    precond_res, res_dot = precondition(residual)
    direction = precond_res
    update = jnp.zeros_like(residual)
    for iteration in range(ITERS):
        image_rows = apply_rows(direction)
        hess_dir = (
            apply_columns((hessian_diag * image_rows).astype(jnp.bfloat16))
            + lambdas[:, None] * direction
        )
        curvature = lax.psum(jnp.sum(direction * hess_dir, axis=1), ("samp", "feat"))
        step_size = res_dot / curvature
        update = update + step_size[:, None] * direction
        if iteration + 1 < ITERS:
            residual = residual - step_size[:, None] * hess_dir
            precond_res, new_dot = precondition(residual)
            direction = precond_res + (new_dot / res_dot)[:, None] * direction
            res_dot = new_dot
    return weights + update


def solution(mesh):
    return jax.shard_map(
        shards,
        mesh=mesh,
        in_specs=(
            P("samp", "feat"),
            P("samp"),
            P(None, ("feat", "samp")),
            P(),
            P(("feat", "samp"), None),
            P(),
        ),
        out_specs=P(None, ("feat", "samp")),
        check_vma=False,
    )
```

profile of v0, /device:TPU:0, one launch (start us, length us, event | category | flops | bytes accessed | tf_op | source)
XLA Modules:
  0.0 595.5 jit_solution(18189731865618623638)
XLA Ops:
  6.5 0.7 convert_element_type.24
  7.3 0.8 convert_element_type.23
  8.1 45.3 %all_gather.9 = bf16[16,16384]{1,0:T(8,128)(2,1)S(1)} all-gather(bf16[16,1024]{1,0:T(8,128)(2,1)S(1)} %convert_element_type.23), channel_id=1, replica_groups=mesh['samp'=16,'feat'=2] {'samp'}, dimensions={1}, use_global_device_ids=true | all-gather | bytes 557056 | tf_op jit(solution)/shard_map/all_gather | solution.py:17
  53.4 3.4 fusion.22
  56.8 2.6 psum.63
  59.5 3.8 convolution_bitcast_fusion.2
  63.4 0.6 reduce_min.9
  64.0 0.6 broadcast_add_fusion
  64.6 73.4 %reduce-scatter.4.cloned.1.call-done = f32[1024,16]{0,1:T(8,128)} async-done(((f32[16384,16]{0,1:T(8,128)}), f32[1024,16]{0,1:T(8,128)}) %reduce-scatter.4.cloned.1.call-update) | async-done | bytes 65552 | tf_op jit(solution)/shard_map/reduce_scatter | solution.py:25
  138.1 0.9 fusion.2
  139.0 0.4 fusion.23
  139.4 37.1 %psum.64 = f32[16,384]{1,0:T(8,128)S(1)} all-reduce(f32[16,384]{1,0:T(8,128)S(1)} %fusion.23), channel_id=1, replica_groups=mesh['samp'=16,'feat'=2] {'samp','feat'}, use_global_device_ids=true, to_apply=%region_3.0 | all-reduce | flops 6144 | bytes 49152 | tf_op jit(solution)/shard_map/psum | solution.py:36
  176.5 0.7 fusion.21
  177.2 41.8 %all_gather.10 = bf16[16,16384]{1,0:T(8,128)(2,1)S(1)} all-gather(bf16[16,1024]{1,0:T(8,128)(2,1)S(1)} %get-tuple-element.9), channel_id=1, replica_groups=mesh['samp'=16,'feat'=2] {'samp'}, dimensions={1}, use_global_device_ids=true | all-gather | bytes 557056 | tf_op jit(solution)/shard_map/all_gather | solution.py:17
  219.0 3.4 fusion.24
  222.3 2.5 psum.66
  224.8 3.8 convolution_bitcast_fusion.1
  228.7 74.6 %reduce-scatter.6.cloned.1.call-done = f32[1024,16]{0,1:T(8,128)} async-done(((f32[16384,16]{0,1:T(8,128)}), f32[1024,16]{0,1:T(8,128)}) %reduce-scatter.6.cloned.1.call-update) | async-done | bytes 65552 | tf_op jit(solution)/shard_map/reduce_scatter | solution.py:25
  303.4 1.0 multiply_reduce_fusion.1
  304.4 36.9 %all-reduce = (f32[16]{0:T(128)S(1)}, f32[16]{0:T(128)S(1)}) all-reduce(f32[16]{0:T(128)S(1)} %get-tuple-element.6, f32[16]{0:T(128)S(1)} %get-tuple-element.5), channel_id=1, replica_groups=mesh['samp'=16,'feat'=2] {'samp','feat'}, use_global_device_ids=true, to_apply=%region_5.0 | all-reduce | flops 32 | bytes 256 | tf_op jit(solution)/shard_map/psum | solution.py:44
  341.3 0.9 multiply_subtract_fusion
  342.6 41.2 %psum.68 = f32[16,384]{1,0:T(8,128)S(1)} all-reduce(f32[16,384]{1,0:T(8,128)S(1)} %fusion.25), channel_id=1, replica_groups=mesh['samp'=16,'feat'=2] {'samp','feat'}, use_global_device_ids=true, to_apply=%region_10.0 | all-reduce | flops 6144 | bytes 49152 | tf_op jit(solution)/shard_map/psum | solution.py:36
  383.8 0.8 multiply_reduce_fusion
  384.7 39.7 %psum.69 = f32[16]{0:T(128)S(1)} all-reduce(f32[16]{0:T(128)S(1)} %get-tuple-element.11), channel_id=1, replica_groups=mesh['samp'=16,'feat'=2] {'samp','feat'}, use_global_device_ids=true, to_apply=%region_12.0 | all-reduce | flops 16 | bytes 128 | tf_op jit(solution)/shard_map/psum | solution.py:44
  424.5 41.5 %all_gather.11 = bf16[16,16384]{1,0:T(8,128)(2,1)S(1)} all-gather(bf16[16,1024]{1,0:T(8,128)(2,1)S(1)} %fusion.20), channel_id=1, replica_groups=mesh['samp'=16,'feat'=2] {'samp'}, dimensions={1}, use_global_device_ids=true | all-gather | bytes 557056 | tf_op jit(solution)/shard_map/all_gather | solution.py:17
  466.0 3.4 fusion.26
  469.3 2.5 psum.70
  471.8 3.9 convolution_bitcast_fusion
  475.7 74.7 %reduce-scatter.8.cloned.1.call-done = f32[1024,16]{0,1:T(8,128)} async-done(((f32[16384,16]{0,1:T(8,128)}), f32[1024,16]{0,1:T(8,128)}) %reduce-scatter.8.cloned.1.call-update) | async-done | bytes 65552 | tf_op jit(solution)/shard_map/reduce_scatter | solution.py:25
  550.4 1.0 fusion.1
  551.4 36.9 %psum.71 = f32[16]{0:T(128)S(1)} all-reduce(f32[16]{0:T(128)S(1)} %fusion.1), channel_id=1, replica_groups=mesh['samp'=16,'feat'=2] {'samp','feat'}, use_global_device_ids=true, to_apply=%region_16.0 | all-reduce | flops 16 | bytes 128 | tf_op jit(solution)/shard_map/psum | solution.py:62
  588.3 0.7 add_add_fusion
  (19 shorter events, 0.7 us)
Async XLA Ops:
  6.5 132.5 %copy-start = (bf16[1024,384]{1,0:T(8,128)(2,1)S(1)}, bf16[1024,384]{1,0:T(8,128)(2,1)}, u32[]{:S(2)}) copy-start(bf16[1024,384]{1,0:T(8,128)(2,1)} %param.10) | copy-start | bytes 2359300
  6.5 131.5 %reduce-scatter.4.cloned.1.call-start = ((), (), s32[]{:S(2)}) async-start(), calls=%async_computation.3 | async-start | bytes 1114112 | tf_op jit(solution)/shard_map/reduce_scatter | solution.py:25
  56.8 6.6 %copy-start.3 = (f32[384]{0:T(512)S(1)}, f32[384]{0:T(512)}, u32[]{:S(2)}) copy-start(f32[384]{0:T(512)} %param.11) | copy-start | bytes 4612
  56.8 7.2 %copy-start.2 = (f32[16]{0:T(128)S(1)}, f32[16]{0:T(128)}, u32[]{:S(2)}) copy-start(f32[16]{0:T(128)} %param.9) | copy-start | bytes 196
  56.8 81.3 %copy-start.1 = (f32[16,1024]{1,0:T(8,128)S(1)}, f32[16,1024]{1,0:T(8,128)}, u32[]{:S(2)}) copy-start(f32[16,1024]{1,0:T(8,128)} %param.8) | copy-start | bytes 196612
  63.3 240.1 %reduce-scatter.6.cloned.1.call-start = ((), (), s32[]{:S(2)}) async-start(), calls=%async_computation.4 | async-start | bytes 1114112 | tf_op jit(solution)/shard_map/reduce_scatter | solution.py:25
  228.7 321.7 %reduce-scatter.8.cloned.1.call-start = ((), (), s32[]{:S(2)}) async-start(), calls=%async_computation.5 | async-start | bytes 1114112 | tf_op jit(solution)/shard_map/reduce_scatter | solution.py:25
Sparse Core Ops, SparseCore 0:
  63.4 74.5 reduce-scatter.3
  228.8 74.5 reduce-scatter.5
  475.8 74.4 reduce-scatter.7
where the time goes:
time: 597 us; the launch traced here: 596 us
  blocking collectives  328 us (55%)
  waiting for transfers between devices  223 us (37%)
  matrix products  24.1 us (4%)
  between operations  13.2 us (2%)
  other arithmetic  7.54 us (1%)
    reduce_scatter x3, waiting for transfers between devices, apply_columns(): lax.psum_scatter(lax.dot_general(design_matrix, values, (((0,), (1,)), ((...  223 us
    all_gather x3, blocking collectives, apply_rows(): lax.all_gather(vector_half, 'samp', axis=1, tiled=True)  129 us
    psum x2, blocking collectives, precondition(): projected = lax.psum(projected, ('samp', 'feat'))  78.2 us
    psum x2, blocking collectives, precondition(): lax.psum(jnp.sum(residual * precond_res, axis=1), ('samp', 'feat'))  76.6 us
    psum x1, blocking collectives, shards(): lax.psum(jnp.sum(direction * hess_dir, axis=1), ('samp', 'feat'))  36.9 us
  transfers between devices with their start and end apart: 3, of which 3 were waited for; matrix products, arithmetic and copies ran while one was open for 0% of the time, Pallas kernels for 0%

commit v1 on v0

--- a/solution.py
+++ b/solution.py
@@ -1,6 +1,10 @@
+import functools
+
 import jax
 import jax.numpy as jnp
 from jax import lax
+from jax.experimental import pallas as pl
+from jax.experimental.pallas import tpu as pltpu
 from jax.sharding import PartitionSpec as P
 
 ITERS = 2
@@ -70,9 +74,353 @@
     return weights + update
 
 
+MESH = pl.DeviceIdType.MESH
+LANES = 128
+PLANE = 4
+
+
+def lane_sums(values):
+    total = values[:, :LANES]
+    for start in range(LANES, values.shape[1], LANES):
+        total = total + values[:, start : start + LANES]
+    return total
+
+
+def split(values):
+    high = values.astype(jnp.bfloat16)
+    low = (values - high.astype(jnp.float32)).astype(jnp.bfloat16)
+    return jnp.concatenate([high, low], axis=0)
+
+
+def kernel(
+    n, feats, design_hbm, labels, weights, lambdas, sketch_hbm, sketch_values, out,
+    design, sketch, gathered, summed, arrived, rows_mine, rows_theirs,
+    proj_mine, proj_theirs, proj_full, plane_mine, plane_theirs, line_mine, line_theirs,
+    curve, design_sem, sketch_sem, gather_sems, sum_sems, row_sems, proj_sems,
+    plane_sems, line_sems, back_sems, curve_sems,
+):
+    me = lax.axis_index("samp")
+    side = lax.axis_index("feat")
+    strengths, width = weights.shape
+    rank = sketch.shape[1]
+    band = strengths // feats
+    planes = n // PLANE
+
+    def fetch(chunk):
+        return pltpu.make_async_copy(
+            design_hbm.at[:, pl.ds(chunk * width, width)], design.at[chunk], design_sem.at[chunk]
+        )
+
+    for chunk in range(n):
+        fetch(chunk).start()
+    sketch_copy = pltpu.make_async_copy(sketch_hbm, sketch, sketch_sem)
+    sketch_copy.start()
+
+    def put(source, target, sems, slot, samp, feat):
+        return pltpu.make_async_remote_copy(
+            src_ref=source, dst_ref=target,
+            send_sem=sems.at[(0, *slot)], recv_sem=sems.at[(1, *slot)],
+            device_id=(samp, feat), device_id_type=MESH,
+        )
+
+    barrier = pltpu.get_barrier_semaphore()
+    for step in range(1, n):
+        pl.semaphore_signal(
+            barrier, inc=1, device_id=(lax.rem(me + step, n), side), device_id_type=MESH
+        )
+    for step in range(1, feats):
+        pl.semaphore_signal(
+            barrier, inc=1, device_id=(me, lax.rem(side + step, feats)), device_id_type=MESH
+        )
+    gathered[0, me] = weights[...].astype(jnp.bfloat16)
+    pl.semaphore_wait(barrier, n - 1 + feats - 1)
+
+    def ahead(step):
+        return lax.rem(me + step, n)
+
+    def behind(step):
+        return lax.rem(me + n - step, n)
+
+    def apply_rows(phase):
+        def copy(step):
+            own = gathered.at[phase, me]
+            return put(own, own, gather_sems, (phase, step), ahead(step), side)
+
+        def multiply(chunk, carry):
+            rows, squares = carry
+            if phase == 0:
+                fetch(chunk).wait()
+            block = gathered[phase, chunk]
+            rows = rows + lax.dot_general(
+                block, design[chunk], (((1,), (1,)), ((), ())), preferred_element_type=jnp.float32
+            )
+            if phase > 0:
+                block = block.astype(jnp.float32)
+                squares = squares + lane_sums(block * block)
+            return rows, squares
+
+        for step in range(1, n):
+            copy(step).start()
+        zero = jnp.zeros((strengths, LANES), jnp.float32)
+        carry = (jnp.zeros((strengths, design.shape[1]), jnp.float32), zero)
+        carry = multiply(me, carry)
+
+        def body(step, carry):
+            copy(step).wait_recv()
+            return multiply(behind(step), carry)
+
+        rows, squares = lax.fori_loop(1, n, body, carry)
+        rows_mine[phase, 0] = rows
+        rows_mine[phase, 1] = squares
+
+        def swap(step):
+            return put(
+                rows_mine.at[phase], rows_theirs.at[phase, step], row_sems, (phase, step),
+                me, lax.rem(side + step, feats),
+            )
+
+        for step in range(1, feats):
+            swap(step).start()
+        for step in range(1, feats):
+            swap(step).wait()
+            rows = rows + rows_theirs[phase, step, 0]
+            squares = squares + rows_theirs[phase, step, 1]
+        for step in range(1, n):
+            copy(step).wait_send()
+        return rows, jnp.sum(squares, axis=1, keepdims=True)
+
+    def apply_columns(phase, values):
+        def copy(step):
+            return put(
+                summed.at[phase, step], arrived.at[phase, step], sum_sems, (phase, step),
+                ahead(step), side,
+            )
+
+        def multiply(chunk):
+            return jnp.dot(values, design[chunk], preferred_element_type=jnp.float32)
+
+        def send(step, _):
+            summed[phase, step] = multiply(ahead(step)).astype(summed.dtype)
+            copy(step).start()
+            return 0
+
+        lax.fori_loop(1, n, send, 0)
+
+        def take(step, total):
+            copy(step).wait()
+            return total + arrived[phase, step].astype(jnp.float32)
+
+        return lax.fori_loop(1, n, take, multiply(me))
+
+    def project(phase, residual):
+        if phase == 0:
+            sketch_copy.wait()
+        parts = jnp.dot(split(residual), sketch[...], preferred_element_type=jnp.float32)
+        total = jnp.concatenate(
+            [parts[:strengths] + parts[strengths:], lane_sums(residual * residual)], axis=1
+        )
+        for step in range(feats):
+            proj_mine[phase, step] = total[step * band : (step + 1) * band]
+
+        def swap(step):
+            other = lax.rem(side + step, feats)
+            return put(
+                proj_mine.at[phase, other], proj_theirs.at[phase, step], proj_sems,
+                (phase, step), me, other,
+            )
+
+        for step in range(1, feats):
+            swap(step).start()
+        part = proj_mine[phase, side]
+        for step in range(1, feats):
+            swap(step).wait()
+            part = part + proj_theirs[phase, step]
+
+        plane_mine[phase] = part
+        corner = me // PLANE * PLANE
+
+        def across(step):
+            return put(
+                plane_mine.at[phase], plane_theirs.at[phase, step], plane_sems, (phase, step),
+                corner + lax.rem(me - corner + step, PLANE), side,
+            )
+
+        for step in range(1, PLANE):
+            across(step).start()
+        for step in range(1, PLANE):
+            across(step).wait()
+            part = part + plane_theirs[phase, step]
+
+        line_mine[phase] = part
+
+        def along(step):
+            return put(
+                line_mine.at[phase], line_theirs.at[phase, step], line_sems, (phase, step),
+                lax.rem(me + step * PLANE, n), side,
+            )
+
+        for step in range(1, planes):
+            along(step).start()
+        for step in range(1, planes):
+            along(step).wait()
+            part = part + line_theirs[phase, step]
+
+        proj_full[phase, side] = part
+
+        def back(step):
+            return put(
+                proj_full.at[phase, side], proj_full.at[phase, side], back_sems, (phase, step),
+                me, lax.rem(side + step, feats),
+            )
+
+        for step in range(1, feats):
+            back(step).start()
+        for step in range(1, feats):
+            other = lax.rem(side + feats - step, feats)
+            put(
+                proj_full.at[phase, other], proj_full.at[phase, other], back_sems, (phase, step),
+                me, other,
+            ).wait_recv()
+        for step in range(1, feats):
+            back(step).wait_send()
+        total = jnp.concatenate([proj_full[phase, step] for step in range(feats)], axis=0)
+        return total[:, :rank], jnp.sum(total[:, rank:], axis=1, keepdims=True)
+
+    def precondition(phase, residual):
+        projected, norm = project(phase, residual)
+        weighted = ratios * projected
+        parts = lax.dot_general(
+            split(weighted), sketch[...], (((1,), (1,)), ((), ())),
+            preferred_element_type=jnp.float32,
+        )
+        res_dot = norm + jnp.sum(weighted * projected, axis=1, keepdims=True)
+        return residual + parts[:strengths] + parts[strengths:], res_dot
+
+    diagonal = (
+        lax.broadcasted_iota(jnp.int32, (strengths, LANES), 0)
+        == lax.broadcasted_iota(jnp.int32, (strengths, LANES), 1)
+    ).astype(jnp.float32)
+
+    def share(phase, values):
+        column = jnp.sum(values, axis=1, keepdims=True)
+        curve[phase, 0] = jnp.sum(column * diagonal, axis=0, keepdims=True)
+
+        def copy(step):
+            return put(
+                curve.at[phase, 0], curve.at[phase, step], curve_sems, (phase, step),
+                ahead(step), side,
+            )
+
+        for step in range(1, n):
+            copy(step).start()
+        return copy
+
+    def collect(phase, copy):
+        for step in range(1, n):
+            copy(step).wait()
+        total = curve[phase, 0]
+        for step in range(1, n):
+            total = total + curve[phase, step]
+        return jnp.sum(total * diagonal, axis=1, keepdims=True)
+
+    strength = lambdas[...]
+    spectrum = sketch_values[...]
+    smallest = jnp.min(spectrum, axis=1, keepdims=True)
+    ratios = (smallest + strength) / (spectrum + strength) - 1.0
+
+    logits, _ = apply_rows(0)
+    probability = jax.nn.sigmoid(logits)
+    hessian_diag = probability * (1.0 - probability)
+    miss_rows = (probability - labels[...].astype(jnp.float32)).astype(jnp.bfloat16)
+    residual = -(apply_columns(0, miss_rows) + strength * weights[...])
+    direction, res_dot = precondition(0, residual)
+    update = jnp.zeros_like(residual)
+    for iteration in range(ITERS):
+        gathered[iteration + 1, me] = direction.astype(jnp.bfloat16)
+        image, squares = apply_rows(iteration + 1)
+        bent = (hessian_diag * image).astype(jnp.bfloat16)
+        copy = share(iteration, bent.astype(jnp.float32) * image)
+        last = iteration + 1 == ITERS
+        if not last:
+            hess_dir = apply_columns(iteration + 1, bent) + strength * direction
+        curvature = collect(iteration, copy) + strength * squares
+        step_size = res_dot / curvature
+        update = update + step_size * direction
+        if not last:
+            residual = residual - step_size * hess_dir
+            precond_res, new_dot = precondition(iteration + 1, residual)
+            direction = precond_res + (new_dot / res_dot) * direction
+            res_dot = new_dot
+    out[...] = weights[...] + update
+
+
+def fused(n, feats, design_matrix, labels, weights, lambdas, sketch, sketch_values):
+    strengths, width = weights.shape
+    samples = design_matrix.shape[0]
+    rank = sketch.shape[1]
+    band = (strengths // feats, rank + LANES)
+    dma = pltpu.SemaphoreType.DMA
+    f32, bf16 = jnp.float32, jnp.bfloat16
+    vmem = pl.BlockSpec(memory_space=pltpu.VMEM)
+    anywhere = pl.BlockSpec(memory_space=pl.ANY)
+    return pl.pallas_call(
+        functools.partial(kernel, n, feats),
+        out_shape=jax.ShapeDtypeStruct(weights.shape, f32),
+        in_specs=[anywhere, vmem, vmem, vmem, anywhere, vmem],
+        out_specs=vmem,
+        scratch_shapes=[
+            pltpu.VMEM((n, samples, width), bf16),
+            pltpu.VMEM(sketch.shape, bf16),
+            pltpu.VMEM((ITERS + 1, n, strengths, width), bf16),
+            pltpu.VMEM((ITERS, n, strengths, width), bf16),
+            pltpu.VMEM((ITERS, n, strengths, width), bf16),
+            pltpu.VMEM((ITERS + 1, 2, strengths, samples), f32),
+            pltpu.VMEM((ITERS + 1, feats, 2, strengths, samples), f32),
+            pltpu.VMEM((ITERS, feats, *band), f32),
+            pltpu.VMEM((ITERS, feats, *band), f32),
+            pltpu.VMEM((ITERS, feats, *band), f32),
+            pltpu.VMEM((ITERS, *band), f32),
+            pltpu.VMEM((ITERS, PLANE, *band), f32),
+            pltpu.VMEM((ITERS, *band), f32),
+            pltpu.VMEM((ITERS, n // PLANE, *band), f32),
+            pltpu.VMEM((ITERS, n, 1, LANES), f32),
+            dma((n,)),
+            dma,
+            dma((2, ITERS + 1, n)),
+            dma((2, ITERS, n)),
+            dma((2, ITERS + 1, feats)),
+            dma((2, ITERS, feats)),
+            dma((2, ITERS, PLANE)),
+            dma((2, ITERS, n // PLANE)),
+            dma((2, ITERS, feats)),
+            dma((2, ITERS, n)),
+        ],
+        compiler_params=pltpu.CompilerParams(
+            collective_id=0, has_side_effects=True, vmem_limit_bytes=48 * 1024 * 1024
+        ),
+    )(
+        design_matrix, labels[None, :], weights, lambdas[:, None], sketch, sketch_values[None, :]
+    )
+
+
 def solution(mesh):
+    n, feats = mesh.shape["samp"], mesh.shape["feat"]
+
+    def local(design_matrix, labels, weights, lambdas, sketch, sketch_values):
+        strengths, width = weights.shape
+        whole = (
+            width % LANES == 0
+            and design_matrix.shape[0] == LANES
+            and sketch.shape[1] % LANES == 0
+            and n % PLANE == 0
+            and strengths % (8 * feats) == 0
+            and strengths <= LANES
+        )
+        run = functools.partial(fused, n, feats) if whole else shards
+        return run(design_matrix, labels, weights, lambdas, sketch, sketch_values)
+
     return jax.shard_map(
-        shards,
+        local,
         mesh=mesh,
         in_specs=(
             P("samp", "feat"),

time: 597 us -> 115 us (0.19)
  blocking collectives: 328 us -> 0 us
  waiting for transfers between devices: 223 us -> 0 us
  Pallas kernels: 0 us -> 108 us
  matrix products: 24.1 us -> 0 us
  between operations: 13.2 us -> 0.01 us
  other arithmetic: 7.54 us -> 0 us
  local copies, waits for them, and re-layouts: 0.03 us -> 6.86 us
    reduce_scatter x3 -> x0, waiting for transfers between devices: 223 us -> none  [apply_columns(): lax.psum_scatter(lax.dot_general(design_matrix, values, (((0,), (1,)), ((...]
    psum x8 -> x0, blocking collectives: 199 us -> none  [the longest x2 78.2 us: precondition(): projected = lax.psum(projected, ('samp', 'feat'))]
    all_gather x3 -> x0, blocking collectives: 129 us -> none  [apply_rows(): lax.all_gather(vector_half, 'samp', axis=1, tiled=True)]
    pallas_call x0 -> x1, Pallas kernels: none -> 108 us  [fused(): pl.pallas_call(functools.partial(kernel, n, feats), out_shape=jax.ShapeDt...]
    dot_general x10 -> x0, matrix products: 24.1 us -> none  [the longest x3 11.5 us: apply_columns(): lax.dot_general(design_matrix, values, (((0,), (1,)), ((), ())), preferre...]
  transfers between devices with their start and end apart: 3 -> 0, of which waited for: 3 -> 0; matrix products, arithmetic and copies ran while one was open for 0% -> 0% of each run, Pallas kernels for 0% -> 0%
where the time goes in v1:
time: 115 us; the launch traced here: 114 us
  Pallas kernels  108 us (94%)
  local copies, waits for them, and re-layouts  6.86 us (6%)
    pallas_call x1, Pallas kernels, fused(): pl.pallas_call(functools.partial(kernel, n, feats), out_shape=jax.ShapeDt...  108 us
    unnamed x9, local copies, waits for them, and re-layouts  5.45 us

profile of v1, /device:TPU:0, one launch (start us, length us, event | category | flops | bytes accessed | tf_op | source)
XLA Modules:
  0.0 114.5 jit_solution(6526984559668552658)
XLA Ops:
  0.0 0.7 broadcast_in_dim.11.sketch_values
  0.7 0.7 copy.7.lambdas
  1.4 0.0 copy-start
  1.4 2.2 %copy-done = bf16[128,16384]{1,0:T(8,128)(2,1)S(1)} copy-done((bf16[128,16384]{1,0:T(8,128)(2,1)S(1)}, bf16[128,16384]{1,0:T(8,128)(2,1)}, u32[]{:S(2)}) %copy-start) | copy-done | bytes 4194328
  3.6 0.0 copy-start.1
  3.6 1.1 copy-done.1
  4.7 0.0 copy-start.2
  4.7 0.8 copy-done.2
  5.6 0.0 copy-start.3
  5.6 0.7 copy-done.3
  6.2 107.6 %shard_map.64 = f32[16,1024]{1,0:T(8,128)S(1)} custom-call(bf16[128,16384]{1,0:T(8,128)(2,1)S(1)} %copy-done, s32[1,128]{1,0:T(1,128)S(1)} %bitcast.2, f32[16,1024]{1,0:T(8,128)S(1)} %copy-done.2, f32[16,1]{1,0:T(8,128)S(1)} %copy.7.lambdas, bf16[1024,384]{1,0:T(8,128)(2,1)S(1)} %copy-done.1, f32[1,384]{1,0:T(1,128)S(1)} %broadcast_in_dim.11.sketch_values), custom_call_target="tpu_custom_call" | custom-call | tf_op jit(solution)/shard_map/pallas_call | solution.py:366
  113.9 0.6 copy.9
Async XLA Ops:
  1.4 2.2 %copy-start = (bf16[128,16384]{1,0:T(8,128)(2,1)S(1)}, bf16[128,16384]{1,0:T(8,128)(2,1)}, u32[]{:S(2)}) copy-start(bf16[128,16384]{1,0:T(8,128)(2,1)} %design_hbm.1) | copy-start | bytes 12582916
  3.6 1.1 copy-start.1
  4.7 0.8 copy-start.2
  5.6 0.7 copy-start.3

commit v2 on v1

--- a/solution.py
+++ b/solution.py
@@ -94,7 +94,7 @@
 
 def kernel(
     n, feats, design_hbm, labels, weights, lambdas, sketch_hbm, sketch_values, out,
-    design, sketch, gathered, summed, arrived, rows_mine, rows_theirs,
+    design, sketch, gathered, half_mine, half_theirs, summed, arrived, rows_mine, rows_theirs,
     proj_mine, proj_theirs, proj_full, plane_mine, plane_theirs, line_mine, line_theirs,
     curve, design_sem, sketch_sem, gather_sems, sum_sems, row_sems, proj_sems,
     plane_sems, line_sems, back_sems, curve_sems,
@@ -138,13 +138,28 @@
     def ahead(step):
         return lax.rem(me + step, n)
 
-    def behind(step):
-        return lax.rem(me + n - step, n)
+    column = lax.rem(me, 2)
+    line = lax.rem(me // 2, 2)
+    beside = me + 1 - 2 * column
+    below = me + 2 - 4 * line
+    across = beside + 2 - 4 * line
+    half = width // 2
+
+    def at(place, step):
+        return lax.rem(place + step * PLANE, n)
 
     def apply_rows(phase):
-        def copy(step):
-            own = gathered.at[phase, me]
-            return put(own, own, gather_sems, (phase, step), ahead(step), side)
+        copies = []
+
+        def send(chunk, kind, step, target, part=slice(None)):
+            block = gathered.at[phase, chunk, :, part]
+            copy = put(block, block, gather_sems, (phase, kind, step), target, side)
+            copy.start()
+            copies.append(copy)
+
+        def receive(chunk, kind, step, part=slice(None)):
+            block = gathered.at[phase, chunk, :, part]
+            put(block, block, gather_sems, (phase, kind, step), beside, side).wait_recv()
 
         def multiply(chunk, carry):
             rows, squares = carry
@@ -159,17 +174,35 @@
                 squares = squares + lane_sums(block * block)
             return rows, squares
 
-        for step in range(1, n):
-            copy(step).start()
+        left, right = slice(0, half), slice(half, width)
+        send(me, 0, 0, beside)
+        send(me, 1, 0, below)
+        for step in range(1, planes):
+            send(me, 4, step, at(me, step))
         zero = jnp.zeros((strengths, LANES), jnp.float32)
         carry = (jnp.zeros((strengths, design.shape[1]), jnp.float32), zero)
         carry = multiply(me, carry)
-
-        def body(step, carry):
-            copy(step).wait_recv()
-            return multiply(behind(step), carry)
-
-        rows, squares = lax.fori_loop(1, n, body, carry)
+        for step in range(planes):
+            if step + 1 < planes:
+                chunk = at(me, planes - step - 1)
+                receive(chunk, 4, step + 1)
+                send(chunk, 0, step + 1, beside)
+                send(chunk, 1, step + 1, below)
+                carry = multiply(chunk, carry)
+            chunk = at(beside, planes - step)
+            receive(chunk, 0, step)
+            send(chunk, 2, step, below, left)
+            other = at(below, planes - step)
+            receive(other, 1, step)
+            send(other, 3, step, beside, right)
+            carry = multiply(chunk, carry)
+            carry = multiply(other, carry)
+        for step in range(planes):
+            chunk = at(across, planes - step)
+            receive(chunk, 2, step, left)
+            receive(chunk, 3, step, right)
+            carry = multiply(chunk, carry)
+        rows, squares = carry
         rows_mine[phase, 0] = rows
         rows_mine[phase, 1] = squares
 
@@ -185,32 +218,76 @@
             swap(step).wait()
             rows = rows + rows_theirs[phase, step, 0]
             squares = squares + rows_theirs[phase, step, 1]
-        for step in range(1, n):
-            copy(step).wait_send()
+        for copy in copies:
+            copy.wait_send()
         return rows, jnp.sum(squares, axis=1, keepdims=True)
 
+    def encode(values):
+        return (values * values * values).astype(jnp.bfloat16)
+
+    def decode(values):
+        values = values.astype(jnp.float32)
+        root = jnp.exp(jnp.log(jnp.abs(values)) * (1.0 / 3.0))
+        return jnp.where(values < 0, -root, root)
+
     def apply_columns(phase, values):
-        def copy(step):
-            return put(
-                summed.at[phase, step], arrived.at[phase, step], sum_sems, (phase, step),
-                ahead(step), side,
+        def halves(kind, step, target):
+            return put(
+                half_mine.at[phase, kind, step], half_theirs.at[phase, kind, step], sum_sems,
+                (phase, kind, step), target, side,
+            )
+
+        def blocks(kind, step, target):
+            return put(
+                summed.at[phase, kind, step], arrived.at[phase, kind, step], sum_sems,
+                (phase, 2 + kind, step), target, side,
             )
 
         def multiply(chunk):
             return jnp.dot(values, design[chunk], preferred_element_type=jnp.float32)
 
-        def send(step, _):
-            summed[phase, step] = multiply(ahead(step)).astype(summed.dtype)
-            copy(step).start()
-            return 0
-
-        lax.fori_loop(1, n, send, 0)
-
-        def take(step, total):
-            copy(step).wait()
-            return total + arrived[phase, step].astype(jnp.float32)
-
-        return lax.fori_loop(1, n, take, multiply(me))
+        steps = (*range(1, planes), 0)
+        for step in steps:
+            part = encode(multiply(at(across, step)))
+            half_mine[phase, 0, step] = part[:, :half]
+            half_mine[phase, 1, step] = part[:, half:]
+            halves(0, step, beside).start()
+            halves(1, step, below).start()
+        for step in steps:
+            part = multiply(at(beside, step))
+            halves(1, step, below).wait_recv()
+            summed[phase, 0, step, :, :half] = encode(part[:, :half])
+            summed[phase, 0, step, :, half:] = encode(
+                part[:, half:] + decode(half_theirs[phase, 1, step])
+            )
+            blocks(0, step, beside).start()
+            part = multiply(at(below, step))
+            halves(0, step, beside).wait_recv()
+            summed[phase, 1, step, :, half:] = encode(part[:, half:])
+            summed[phase, 1, step, :, :half] = encode(
+                part[:, :half] + decode(half_theirs[phase, 0, step])
+            )
+            blocks(1, step, below).start()
+        for step in steps:
+            total = multiply(at(me, step))
+            blocks(0, step, beside).wait_recv()
+            total = total + decode(arrived[phase, 0, step])
+            blocks(1, step, below).wait_recv()
+            total = total + decode(arrived[phase, 1, step])
+            if step > 0:
+                summed[phase, 2, step] = encode(total)
+                blocks(2, step, at(me, step)).start()
+        for step in range(1, planes):
+            blocks(2, step, at(me, step)).wait_recv()
+            total = total + decode(arrived[phase, 2, step])
+        for step in steps:
+            halves(0, step, beside).wait_send()
+            halves(1, step, below).wait_send()
+            blocks(0, step, beside).wait_send()
+            blocks(1, step, below).wait_send()
+            if step > 0:
+                blocks(2, step, at(me, step)).wait_send()
+        return total
 
     def project(phase, residual):
         if phase == 0:
@@ -239,16 +316,16 @@
         plane_mine[phase] = part
         corner = me // PLANE * PLANE
 
-        def across(step):
+        def spread(step):
             return put(
                 plane_mine.at[phase], plane_theirs.at[phase, step], plane_sems, (phase, step),
                 corner + lax.rem(me - corner + step, PLANE), side,
             )
 
         for step in range(1, PLANE):
-            across(step).start()
+            spread(step).start()
         for step in range(1, PLANE):
-            across(step).wait()
+            spread(step).wait()
             part = part + plane_theirs[phase, step]
 
         line_mine[phase] = part
@@ -358,6 +435,7 @@
     strengths, width = weights.shape
     samples = design_matrix.shape[0]
     rank = sketch.shape[1]
+    planes = n // PLANE
     band = (strengths // feats, rank + LANES)
     dma = pltpu.SemaphoreType.DMA
     f32, bf16 = jnp.float32, jnp.bfloat16
@@ -372,8 +450,10 @@
             pltpu.VMEM((n, samples, width), bf16),
             pltpu.VMEM(sketch.shape, bf16),
             pltpu.VMEM((ITERS + 1, n, strengths, width), bf16),
-            pltpu.VMEM((ITERS, n, strengths, width), bf16),
-            pltpu.VMEM((ITERS, n, strengths, width), bf16),
+            pltpu.VMEM((ITERS, 2, planes, strengths, width // 2), bf16),
+            pltpu.VMEM((ITERS, 2, planes, strengths, width // 2), bf16),
+            pltpu.VMEM((ITERS, 3, planes, strengths, width), bf16),
+            pltpu.VMEM((ITERS, 3, planes, strengths, width), bf16),
             pltpu.VMEM((ITERS + 1, 2, strengths, samples), f32),
             pltpu.VMEM((ITERS + 1, feats, 2, strengths, samples), f32),
             pltpu.VMEM((ITERS, feats, *band), f32),
@@ -382,16 +462,16 @@
             pltpu.VMEM((ITERS, *band), f32),
             pltpu.VMEM((ITERS, PLANE, *band), f32),
             pltpu.VMEM((ITERS, *band), f32),
-            pltpu.VMEM((ITERS, n // PLANE, *band), f32),
+            pltpu.VMEM((ITERS, planes, *band), f32),
             pltpu.VMEM((ITERS, n, 1, LANES), f32),
             dma((n,)),
             dma,
-            dma((2, ITERS + 1, n)),
-            dma((2, ITERS, n)),
+            dma((2, ITERS + 1, 5, planes)),
+            dma((2, ITERS, 5, planes)),
             dma((2, ITERS + 1, feats)),
             dma((2, ITERS, feats)),
             dma((2, ITERS, PLANE)),
-            dma((2, ITERS, n // PLANE)),
+            dma((2, ITERS, planes)),
             dma((2, ITERS, feats)),
             dma((2, ITERS, n)),
         ],
@@ -409,7 +489,7 @@
     def local(design_matrix, labels, weights, lambdas, sketch, sketch_values):
         strengths, width = weights.shape
         whole = (
-            width % LANES == 0
+            width % (2 * LANES) == 0
             and design_matrix.shape[0] == LANES
             and sketch.shape[1] % LANES == 0
             and n % PLANE == 0

time: 115 us -> 104 us (0.904)
  Pallas kernels: 108 us -> 96.6 us
    pallas_call x1, Pallas kernels: 108 us -> 96.6 us  [fused(): pl.pallas_call(functools.partial(kernel, n, feats), out_shape=jax.ShapeDt...]
where the time goes in v2:
time: 104 us; the launch traced here: 103 us
  Pallas kernels  96.6 us (93%)
  local copies, waits for them, and re-layouts  6.86 us (7%)
    pallas_call x1, Pallas kernels, fused(): pl.pallas_call(functools.partial(kernel, n, feats), out_shape=jax.ShapeDt...  96.6 us
    unnamed x9, local copies, waits for them, and re-layouts  5.45 us

profile of v2, /device:TPU:0, one launch (start us, length us, event | category | flops | bytes accessed | tf_op | source)
XLA Modules:
  0.0 103.5 jit_solution(11411550006359340829)
XLA Ops:
  0.0 0.7 broadcast_in_dim.11.sketch_values
  0.7 0.7 copy.7.lambdas
  1.4 0.0 copy-start
  1.4 2.2 %copy-done = bf16[128,16384]{1,0:T(8,128)(2,1)S(1)} copy-done((bf16[128,16384]{1,0:T(8,128)(2,1)S(1)}, bf16[128,16384]{1,0:T(8,128)(2,1)}, u32[]{:S(2)}) %copy-start) | copy-done | bytes 4194328
  3.6 0.0 copy-start.1
  3.6 1.1 %copy-done.1 = bf16[1024,384]{1,0:T(8,128)(2,1)S(1)} copy-done((bf16[1024,384]{1,0:T(8,128)(2,1)S(1)}, bf16[1024,384]{1,0:T(8,128)(2,1)}, u32[]{:S(2)}) %copy-start.1) | copy-done | bytes 786456
  4.7 0.0 copy-start.2
  4.7 0.8 copy-done.2
  5.6 0.0 copy-start.3
  5.6 0.7 copy-done.3
  6.2 96.6 %shard_map.64 = f32[16,1024]{1,0:T(8,128)S(1)} custom-call(bf16[128,16384]{1,0:T(8,128)(2,1)S(1)} %copy-done, s32[1,128]{1,0:T(1,128)S(1)} %bitcast.2, f32[16,1024]{1,0:T(8,128)S(1)} %copy-done.2, f32[16,1]{1,0:T(8,128)S(1)} %copy.7.lambdas, bf16[1024,384]{1,0:T(8,128)(2,1)S(1)} %copy-done.1, f32[1,384]{1,0:T(1,128)S(1)} %broadcast_in_dim.11.sketch_values), custom_call_target="tpu_custom_call" | custom-call | tf_op jit(solution)/shard_map/pallas_call | solution.py:444
  102.8 0.6 copy.9
Async XLA Ops:
  1.4 2.2 %copy-start = (bf16[128,16384]{1,0:T(8,128)(2,1)S(1)}, bf16[128,16384]{1,0:T(8,128)(2,1)}, u32[]{:S(2)}) copy-start(bf16[128,16384]{1,0:T(8,128)(2,1)} %design_hbm.1) | copy-start | bytes 12582916
  3.6 1.1 %copy-start.1 = (bf16[1024,384]{1,0:T(8,128)(2,1)S(1)}, bf16[1024,384]{1,0:T(8,128)(2,1)}, u32[]{:S(2)}) copy-start(bf16[1024,384]{1,0:T(8,128)(2,1)} %sketch_hbm.1) | copy-start | bytes 2359300
  4.7 0.8 copy-start.2
  5.6 0.7 copy-start.3

commit v3 on v2

--- a/solution.py
+++ b/solution.py
@@ -93,10 +93,10 @@
 
 
 def kernel(
-    n, feats, design_hbm, labels, weights, lambdas, sketch_hbm, sketch_values, out,
-    design, sketch, gathered, half_mine, half_theirs, summed, arrived, rows_mine, rows_theirs,
+    n, feats, design_hbm, labels_hbm, weights_hbm, lambdas_hbm, sketch_hbm, values_hbm, out,
+    design, labels, weights, lambdas, sketch, sketch_values, gathered, half_mine, half_theirs, summed, arrived, rows_mine, rows_theirs,
     proj_mine, proj_theirs, proj_full, plane_mine, plane_theirs, line_mine, line_theirs,
-    curve, design_sem, sketch_sem, gather_sems, sum_sems, row_sems, proj_sems,
+    curve, design_sem, sketch_sem, small_sems, gather_sems, sum_sems, row_sems, proj_sems,
     plane_sems, line_sems, back_sems, curve_sems,
 ):
     me = lax.axis_index("samp")
@@ -111,6 +111,15 @@
             design_hbm.at[:, pl.ds(chunk * width, width)], design.at[chunk], design_sem.at[chunk]
         )
 
+    weights_copy = pltpu.make_async_copy(weights_hbm, weights, small_sems.at[0])
+    weights_copy.start()
+    small_copies = (
+        pltpu.make_async_copy(labels_hbm, labels, small_sems.at[1]),
+        pltpu.make_async_copy(lambdas_hbm, lambdas, small_sems.at[2]),
+        pltpu.make_async_copy(values_hbm, sketch_values, small_sems.at[3]),
+    )
+    for copy in small_copies:
+        copy.start()
     for chunk in range(n):
         fetch(chunk).start()
     sketch_copy = pltpu.make_async_copy(sketch_hbm, sketch, sketch_sem)
@@ -122,21 +131,6 @@
             send_sem=sems.at[(0, *slot)], recv_sem=sems.at[(1, *slot)],
             device_id=(samp, feat), device_id_type=MESH,
         )
-
-    barrier = pltpu.get_barrier_semaphore()
-    for step in range(1, n):
-        pl.semaphore_signal(
-            barrier, inc=1, device_id=(lax.rem(me + step, n), side), device_id_type=MESH
-        )
-    for step in range(1, feats):
-        pl.semaphore_signal(
-            barrier, inc=1, device_id=(me, lax.rem(side + step, feats)), device_id_type=MESH
-        )
-    gathered[0, me] = weights[...].astype(jnp.bfloat16)
-    pl.semaphore_wait(barrier, n - 1 + feats - 1)
-
-    def ahead(step):
-        return lax.rem(me + step, n)
 
     column = lax.rem(me, 2)
     line = lax.rem(me // 2, 2)
@@ -145,8 +139,28 @@
     across = beside + 2 - 4 * line
     half = width // 2
 
+    level = me // PLANE
+
     def at(place, step):
-        return lax.rem(place + step * PLANE, n)
+        other, bit = 0, 1
+        while bit < planes:
+            other = other + lax.rem(level // bit + step // bit, 2) * bit
+            bit *= 2
+        return place + (other - level) * PLANE
+
+    barrier = pltpu.get_barrier_semaphore()
+    for partner in (beside, below, across, *(at(me, step) for step in range(1, planes))):
+        pl.semaphore_signal(barrier, inc=1, device_id=(partner, side), device_id_type=MESH)
+    for step in range(1, feats):
+        pl.semaphore_signal(
+            barrier, inc=1, device_id=(me, lax.rem(side + step, feats)), device_id_type=MESH
+        )
+    weights_copy.wait()
+    gathered[0, me] = weights[...].astype(jnp.bfloat16)
+    pl.semaphore_wait(barrier, PLANE - 1 + planes - 1 + feats - 1)
+
+    def ahead(step):
+        return lax.rem(me + step, n)
 
     def apply_rows(phase):
         copies = []
@@ -184,21 +198,21 @@
         carry = multiply(me, carry)
         for step in range(planes):
             if step + 1 < planes:
-                chunk = at(me, planes - step - 1)
+                chunk = at(me, step + 1)
                 receive(chunk, 4, step + 1)
                 send(chunk, 0, step + 1, beside)
                 send(chunk, 1, step + 1, below)
                 carry = multiply(chunk, carry)
-            chunk = at(beside, planes - step)
+            chunk = at(beside, step)
             receive(chunk, 0, step)
             send(chunk, 2, step, below, left)
-            other = at(below, planes - step)
+            other = at(below, step)
             receive(other, 1, step)
             send(other, 3, step, beside, right)
             carry = multiply(chunk, carry)
             carry = multiply(other, carry)
         for step in range(planes):
-            chunk = at(across, planes - step)
+            chunk = at(across, step)
             receive(chunk, 2, step, left)
             receive(chunk, 3, step, right)
             carry = multiply(chunk, carry)
@@ -246,7 +260,7 @@
         def multiply(chunk):
             return jnp.dot(values, design[chunk], preferred_element_type=jnp.float32)
 
-        steps = (*range(1, planes), 0)
+        steps = tuple(reversed(range(planes)))
         for step in steps:
             part = encode(multiply(at(across, step)))
             half_mine[phase, 0, step] = part[:, :half]
@@ -333,7 +347,7 @@
         def along(step):
             return put(
                 line_mine.at[phase], line_theirs.at[phase, step], line_sems, (phase, step),
-                lax.rem(me + step * PLANE, n), side,
+                at(me, step), side,
             )
 
         for step in range(1, planes):
@@ -400,12 +414,13 @@
             total = total + curve[phase, step]
         return jnp.sum(total * diagonal, axis=1, keepdims=True)
 
-    strength = lambdas[...]
-    spectrum = sketch_values[...]
+    logits, _ = apply_rows(0)
+    for copy in small_copies:
+        copy.wait()
+    strength = jnp.sum(lambdas[...] * diagonal[:, :strengths], axis=1, keepdims=True)
+    spectrum = sketch_values[...][None, :]
     smallest = jnp.min(spectrum, axis=1, keepdims=True)
     ratios = (smallest + strength) / (spectrum + strength) - 1.0
-
-    logits, _ = apply_rows(0)
     probability = jax.nn.sigmoid(logits)
     hessian_diag = probability * (1.0 - probability)
     miss_rows = (probability - labels[...].astype(jnp.float32)).astype(jnp.bfloat16)
@@ -444,11 +459,15 @@
     return pl.pallas_call(
         functools.partial(kernel, n, feats),
         out_shape=jax.ShapeDtypeStruct(weights.shape, f32),
-        in_specs=[anywhere, vmem, vmem, vmem, anywhere, vmem],
+        in_specs=[anywhere] * 6,
         out_specs=vmem,
         scratch_shapes=[
             pltpu.VMEM((n, samples, width), bf16),
+            pltpu.VMEM((1, samples), jnp.int32),
+            pltpu.VMEM(weights.shape, f32),
+            pltpu.VMEM((1, strengths), f32),
             pltpu.VMEM(sketch.shape, bf16),
+            pltpu.VMEM(sketch_values.shape, f32),
             pltpu.VMEM((ITERS + 1, n, strengths, width), bf16),
             pltpu.VMEM((ITERS, 2, planes, strengths, width // 2), bf16),
             pltpu.VMEM((ITERS, 2, planes, strengths, width // 2), bf16),
@@ -466,6 +485,7 @@
             pltpu.VMEM((ITERS, n, 1, LANES), f32),
             dma((n,)),
             dma,
+            dma((4,)),
             dma((2, ITERS + 1, 5, planes)),
             dma((2, ITERS, 5, planes)),
             dma((2, ITERS + 1, feats)),
@@ -476,10 +496,10 @@
             dma((2, ITERS, n)),
         ],
         compiler_params=pltpu.CompilerParams(
-            collective_id=0, has_side_effects=True, vmem_limit_bytes=48 * 1024 * 1024
+            collective_id=0, has_side_effects=True, vmem_limit_bytes=63 * 1024 * 1024
         ),
     )(
-        design_matrix, labels[None, :], weights, lambdas[:, None], sketch, sketch_values[None, :]
+        design_matrix, labels[None, :], weights, lambdas[None, :], sketch, sketch_values
     )
 
 
@@ -493,6 +513,7 @@
             and design_matrix.shape[0] == LANES
             and sketch.shape[1] % LANES == 0
             and n % PLANE == 0
+            and n & (n - 1) == 0
             and strengths % (8 * feats) == 0
             and strengths <= LANES
         )

time: 104 us -> 96.9 us (0.932)
  local copies, waits for them, and re-layouts: 6.86 us -> 1.47 us
  Pallas kernels: 96.6 us -> 95.2 us
    unnamed x9 -> x1, local copies, waits for them, and re-layouts: 5.45 us -> 1.47 us
    broadcast_in_dim x2 -> x0, local copies, waits for them, and re-layouts: 1.41 us -> none  [the longest x1 0.73 us: fused(): lambdas[:, None]]
    pallas_call x1, Pallas kernels: 96.6 us -> 95.2 us  [fused(): pl.pallas_call(functools.partial(kernel, n, feats), out_shape=jax.ShapeDt...]
where the time goes in v3:
time: 96.9 us; the launch traced here: 96.7 us
  Pallas kernels  95.2 us (98%)
  local copies, waits for them, and re-layouts  1.47 us (2%)
    pallas_call x1, Pallas kernels, fused(): pl.pallas_call(functools.partial(kernel, n, feats), out_shape=jax.ShapeDt...  95.2 us

profile of v3, /device:TPU:0, one launch (start us, length us, event | category | flops | bytes accessed | tf_op | source)
XLA Modules:
  0.0 96.7 jit_solution(11551977529451444447)
XLA Ops:
  0.0 95.2 %shard_map.64 = f32[16,1024]{1,0:T(8,128)} custom-call(bf16[128,16384]{1,0:T(8,128)(2,1)} %design_hbm.1, s32[1,128]{1,0:T(1,128)} %bitcast.2, f32[16,1024]{1,0:T(8,128)} %weights_hbm.1, f32[1,16]{1,0:T(1,128)} %bitcast.3, bf16[1024,384]{1,0:T(8,128)(2,1)} %sketch_hbm.1, f32[384]{0:T(512)} %values_hbm.1), custom_call_target="tpu_custom_call" | custom-call | tf_op jit(solution)/shard_map/pallas_call | solution.py:459
  95.2 1.5 %copy.8 = f32[16,1024]{1,0:T(8,128)} copy(f32[16,1024]{1,0:T(8,128)} %shard_map.64) | data formatting | bytes 131072

commit v4 on v3

--- a/solution.py
+++ b/solution.py
@@ -138,6 +138,7 @@
     below = me + 2 - 4 * line
     across = beside + 2 - 4 * line
     half = width // 2
+    far = planes - 1
 
     level = me // PLANE
 
@@ -193,6 +194,7 @@
         send(me, 1, 0, below)
         for step in range(1, planes):
             send(me, 4, step, at(me, step))
+        send(me, 2, 0, across)
         zero = jnp.zeros((strengths, LANES), jnp.float32)
         carry = (jnp.zeros((strengths, design.shape[1]), jnp.float32), zero)
         carry = multiply(me, carry)
@@ -203,19 +205,29 @@
                 send(chunk, 0, step + 1, beside)
                 send(chunk, 1, step + 1, below)
                 carry = multiply(chunk, carry)
+            relayed = 0 < step < far
             chunk = at(beside, step)
             receive(chunk, 0, step)
-            send(chunk, 2, step, below, left)
+            if relayed:
+                send(chunk, 2, step, below, left)
             other = at(below, step)
             receive(other, 1, step)
-            send(other, 3, step, beside, right)
+            if relayed:
+                send(other, 3, step, beside, right)
             carry = multiply(chunk, carry)
             carry = multiply(other, carry)
-        for step in range(planes):
+            if step == 0:
+                receive(across, 2, 0)
+                send(across, 4, 0, at(me, far))
+                carry = multiply(across, carry)
+        for step in range(1, far):
             chunk = at(across, step)
             receive(chunk, 2, step, left)
             receive(chunk, 3, step, right)
             carry = multiply(chunk, carry)
+        chunk = at(across, far)
+        receive(chunk, 4, 0)
+        carry = multiply(chunk, carry)
         rows, squares = carry
         rows_mine[phase, 0] = rows
         rows_mine[phase, 1] = squares
@@ -261,26 +273,29 @@
             return jnp.dot(values, design[chunk], preferred_element_type=jnp.float32)
 
         steps = tuple(reversed(range(planes)))
-        for step in steps:
+        middle = steps[1:-1]
+        summed[phase, 3, far] = encode(multiply(at(across, far)))
+        blocks(3, far, at(me, far)).start()
+        for step in middle:
             part = encode(multiply(at(across, step)))
             half_mine[phase, 0, step] = part[:, :half]
             half_mine[phase, 1, step] = part[:, half:]
             halves(0, step, beside).start()
             halves(1, step, below).start()
         for step in steps:
-            part = multiply(at(beside, step))
-            halves(1, step, below).wait_recv()
-            summed[phase, 0, step, :, :half] = encode(part[:, :half])
-            summed[phase, 0, step, :, half:] = encode(
-                part[:, half:] + decode(half_theirs[phase, 1, step])
-            )
+            aside = multiply(at(beside, step))
+            under = multiply(at(below, step))
+            if step in middle:
+                halves(1, step, below).wait_recv()
+                more = decode(half_theirs[phase, 1, step])
+                aside = jnp.concatenate([aside[:, :half], aside[:, half:] + more], axis=1)
+            summed[phase, 0, step] = encode(aside)
             blocks(0, step, beside).start()
-            part = multiply(at(below, step))
-            halves(0, step, beside).wait_recv()
-            summed[phase, 1, step, :, half:] = encode(part[:, half:])
-            summed[phase, 1, step, :, :half] = encode(
-                part[:, :half] + decode(half_theirs[phase, 0, step])
-            )
+            if step in middle:
+                halves(0, step, beside).wait_recv()
+                more = decode(half_theirs[phase, 0, step])
+                under = jnp.concatenate([under[:, :half] + more, under[:, half:]], axis=1)
+            summed[phase, 1, step] = encode(under)
             blocks(1, step, below).start()
         for step in steps:
             total = multiply(at(me, step))
@@ -291,16 +306,26 @@
             if step > 0:
                 summed[phase, 2, step] = encode(total)
                 blocks(2, step, at(me, step)).start()
+            if step == far:
+                part = multiply(across)
+                blocks(3, far, at(me, far)).wait_recv()
+                summed[phase, 3, 0] = encode(part + decode(arrived[phase, 3, far]))
+                blocks(3, 0, across).start()
         for step in range(1, planes):
             blocks(2, step, at(me, step)).wait_recv()
             total = total + decode(arrived[phase, 2, step])
+        blocks(3, 0, across).wait_recv()
+        total = total + decode(arrived[phase, 3, 0])
         for step in steps:
-            halves(0, step, beside).wait_send()
-            halves(1, step, below).wait_send()
+            if step in middle:
+                halves(0, step, beside).wait_send()
+                halves(1, step, below).wait_send()
             blocks(0, step, beside).wait_send()
             blocks(1, step, below).wait_send()
             if step > 0:
                 blocks(2, step, at(me, step)).wait_send()
+        blocks(3, far, at(me, far)).wait_send()
+        blocks(3, 0, across).wait_send()
         return total
 
     def project(phase, residual):
@@ -327,7 +352,8 @@
             swap(step).wait()
             part = part + proj_theirs[phase, step]
 
-        plane_mine[phase] = part
+        plane_mine[phase] = part.astype(jnp.bfloat16)
+        part = plane_mine[phase].astype(jnp.float32)
         corner = me // PLANE * PLANE
 
         def spread(step):
@@ -340,9 +366,10 @@
             spread(step).start()
         for step in range(1, PLANE):
             spread(step).wait()
-            part = part + plane_theirs[phase, step]
-
-        line_mine[phase] = part
+            part = part + plane_theirs[phase, step].astype(jnp.float32)
+
+        line_mine[phase] = part.astype(jnp.bfloat16)
+        part = line_mine[phase].astype(jnp.float32)
 
         def along(step):
             return put(
@@ -354,7 +381,7 @@
             along(step).start()
         for step in range(1, planes):
             along(step).wait()
-            part = part + line_theirs[phase, step]
+            part = part + line_theirs[phase, step].astype(jnp.float32)
 
         proj_full[phase, side] = part
 
@@ -471,23 +498,23 @@
             pltpu.VMEM((ITERS + 1, n, strengths, width), bf16),
             pltpu.VMEM((ITERS, 2, planes, strengths, width // 2), bf16),
             pltpu.VMEM((ITERS, 2, planes, strengths, width // 2), bf16),
-            pltpu.VMEM((ITERS, 3, planes, strengths, width), bf16),
-            pltpu.VMEM((ITERS, 3, planes, strengths, width), bf16),
+            pltpu.VMEM((ITERS, 4, planes, strengths, width), bf16),
+            pltpu.VMEM((ITERS, 4, planes, strengths, width), bf16),
             pltpu.VMEM((ITERS + 1, 2, strengths, samples), f32),
             pltpu.VMEM((ITERS + 1, feats, 2, strengths, samples), f32),
             pltpu.VMEM((ITERS, feats, *band), f32),
             pltpu.VMEM((ITERS, feats, *band), f32),
             pltpu.VMEM((ITERS, feats, *band), f32),
-            pltpu.VMEM((ITERS, *band), f32),
-            pltpu.VMEM((ITERS, PLANE, *band), f32),
-            pltpu.VMEM((ITERS, *band), f32),
-            pltpu.VMEM((ITERS, planes, *band), f32),
+            pltpu.VMEM((ITERS, *band), bf16),
+            pltpu.VMEM((ITERS, PLANE, *band), bf16),
+            pltpu.VMEM((ITERS, *band), bf16),
+            pltpu.VMEM((ITERS, planes, *band), bf16),
             pltpu.VMEM((ITERS, n, 1, LANES), f32),
             dma((n,)),
             dma,
             dma((4,)),
             dma((2, ITERS + 1, 5, planes)),
-            dma((2, ITERS, 5, planes)),
+            dma((2, ITERS, 6, planes)),
             dma((2, ITERS + 1, feats)),
             dma((2, ITERS, feats)),
             dma((2, ITERS, PLANE)),
@@ -513,6 +540,7 @@
             and design_matrix.shape[0] == LANES
             and sketch.shape[1] % LANES == 0
             and n % PLANE == 0
+            and n > PLANE
             and n & (n - 1) == 0
             and strengths % (8 * feats) == 0
             and strengths <= LANES

time: 96.9 us -> 89.4 us (0.923)
  Pallas kernels: 95.2 us -> 87.8 us
    pallas_call x1, Pallas kernels: 95.2 us -> 87.8 us  [fused(): pl.pallas_call(functools.partial(kernel, n, feats), out_shape=jax.ShapeDt...]
where the time goes in v4:
time: 89.4 us; the launch traced here: 89.3 us
  Pallas kernels  87.8 us (98%)
  local copies, waits for them, and re-layouts  1.47 us (2%)
    pallas_call x1, Pallas kernels, fused(): pl.pallas_call(functools.partial(kernel, n, feats), out_shape=jax.ShapeDt...  87.8 us

profile of v4, /device:TPU:0, one launch (start us, length us, event | category | flops | bytes accessed | tf_op | source)
XLA Modules:
  0.0 89.3 jit_solution(10809666462185467944)
XLA Ops:
  0.0 87.8 %shard_map.64 = f32[16,1024]{1,0:T(8,128)} custom-call(bf16[128,16384]{1,0:T(8,128)(2,1)} %design_hbm.1, s32[1,128]{1,0:T(1,128)} %bitcast.2, f32[16,1024]{1,0:T(8,128)} %weights_hbm.1, f32[1,16]{1,0:T(1,128)} %bitcast.3, bf16[1024,384]{1,0:T(8,128)(2,1)} %sketch_hbm.1, f32[384]{0:T(512)} %values_hbm.1), custom_call_target="tpu_custom_call" | custom-call | tf_op jit(solution)/shard_map/pallas_call | solution.py:486
  87.8 1.5 %copy.8 = f32[16,1024]{1,0:T(8,128)} copy(f32[16,1024]{1,0:T(8,128)} %shard_map.64) | data formatting | bytes 131072
